TPU v7x, 32 devices: a whole 2x2x4 slice. The times are simulated.
32 devices in a mesh: grp: 2 (over x), seq: 8 (over z, y), head: 2 (over core).
Axes of the slice: x: 2, y: 2, z: 4, core: 2. Of those that a mesh axis runs over, the one named last changes fastest.
Arguments:
- patches: bfloat16 [3072, 1280], P(('grp', 'seq')), parts along dimension 0, may hold values from -6 to 6
- ln_gain: float32 [1280], replicated, may hold values from 0.25 to 1.75
- ln_bias: float32 [1280], replicated, may hold values from -3 to 3
- qkv_weight: bfloat16 [1280, 3, 1280], P(None, None, 'head'), may hold values from -0.15625 to 0.15625
- proj_weight: bfloat16 [1280, 1280], P('head'), may hold values from -0.15625 to 0.15625
- proj_bias: float32 [1280], replicated, may hold values from -3 to 3
- merge_gain: float32 [1280], replicated, may hold values from 0.25 to 1.75
- merge_bias: float32 [1280], replicated, may hold values from -3 to 3
- visual_kv_weight: bfloat16 [5120, 2, 512], P(None, None, 'head'), may hold values from -0.078125 to 0.078125
- image_tokens: int32 [32], P('grp'), parts along dimension 0, may hold values from 2 to 47, as said below
- text_before: int32 [32], P('grp'), parts along dimension 0, may hold values from 0 to 1024, as said below
- text_order: int32 [2048], P(('grp', 'seq')), parts along dimension 0, may hold values from 0 to 1023, each once
- queries: bfloat16 [2048, 4096], P(('grp', 'seq'), 'head'), parts along dimension 0, may hold values from -44 to 44
- text_kv: bfloat16 [2048, 2, 512], P(('grp', 'seq'), None, 'head'), parts along dimension 0, may hold values from -4 to 4
Outputs:
- attended: bfloat16 [2048, 4096], P(('grp', 'seq'), 'head'), parts along dimension 0
- visual_kv: bfloat16 [768, 2, 512], P(('grp', 'seq'), None, 'head'), parts along dimension 0
There are 2 independent parts, one for each index of `grp`. A program takes and returns all parts, laid end to end along the dimension named above; an argument that names none is the same for every part. Nothing has to cross between parts.
Inputs may be any that keep to these rules, and one draw needn't show every extreme that they name: `image_tokens`: they sum to 384; each run of 48 visual tokens of one index of seq holds the last token of exactly two images (the last index: of one image and of the last image), so an image crosses every boundary between indices; the last image holds 47 tokens. `text_before`: non-decreasing. `text_order`: each number once.
All inputs are finite; a program needn't handle non-finite values.
Results may differ from a plain program's by a relative error of at most 0.0095.
Values may be sent and summed in bfloat16 or wider, within the bound.
No kernel may reach another device: no remote copies, remote signals or barrier semaphores. Data moves between devices by JAX's collectives and lax.ppermute only.
A program may use at most 128 MiB of HBM per device.

v0:
```python
import functools
import math

import jax
import jax.numpy as jnp
from jax import lax
from jax.experimental import pallas as pl
from jax.experimental.pallas import tpu as pltpu
from jax.sharding import PartitionSpec as P


VIT_HD = 80
HEAD_DIM = 128
GROUP = 8
LANES = 128

epsilon = 1e-06
SHIFTS = (2, 4, 6, 1, 7, 3, 5)
masked_score = -1e30


f32 = jnp.float32
bf16 = jnp.bfloat16


def layer_norm(inputs, scale_gain, shift_bias):
    centre = jnp.mean(inputs, axis=-1, keepdims=True)
    centred = inputs - centre
    spread = jnp.mean(centred * centred, axis=-1, keepdims=True)
    return centred * lax.rsqrt(spread + epsilon) * scale_gain + shift_bias


def padded_bytes(shape, dtype):
    item = jnp.dtype(dtype).itemsize
    rows = shape[-2] if len(shape) > 1 else 1
    count = math.prod(shape[:-2]) * (-(-rows // 16) * 16) * (-(-shape[-1] // LANES) * LANES)
    return count * item


def vmem_call(body, out_shape, scratch=(), flops=0, nbytes=0, trans=0, spaces=None, spare=6 << 20, keep=False):
    spaces = spaces or {}

    def run(*args):
        args = [pltpu.with_memory_space_constraint(a, pltpu.HBM) if spaces.get(i) == pltpu.HBM else a for i, a in enumerate(args)]
        multi = isinstance(out_shape, (tuple, list))
        size = sum(padded_bytes(a.shape, a.dtype) for a in scratch if a.memory_space == pltpu.VMEM)
        spec = pl.BlockSpec(memory_space=pltpu.VMEM)
        return pl.pallas_call(
            body,
            out_shape=jax.tree.map(lambda a: pltpu.VMEM(a.shape, a.dtype), out_shape) if keep else out_shape,
            in_specs=[pl.BlockSpec(memory_space=spaces.get(i, pltpu.VMEM)) for i in range(len(args))],
            out_specs=[spec] * len(out_shape) if multi else spec,
            scratch_shapes=scratch,
            compiler_params=pltpu.CompilerParams(vmem_limit_bytes=size + spare),
            cost_estimate=pl.CostEstimate(flops=flops, bytes_accessed=nbytes, transcendentals=trans),
        )(*args)

    return run


def layer_norm_rows(refs, gain_ref, bias_ref):
    width = gain_ref.shape[0]
    rows = jnp.concatenate([ref[...] for ref in refs], axis=0).astype(f32)
    return layer_norm(rows, gain_ref[...].reshape(1, width), bias_ref[...].reshape(1, width)).astype(bf16)


def pick(index, segments):
    out = index + segments[0][1]
    for offset, start in segments[1:]:
        out = jnp.where(index >= offset, index - offset + start, out)
    return out


def prep_kernel(dims, *refs):
    seq_count, small, rows, merged = dims
    sources, outs, held, sem = refs[:4], refs[4:8], refs[8:12], refs[12]
    copies = [pltpu.make_async_copy(a, b, sem.at[i]) for i, (a, b) in enumerate(zip(sources, held))]
    for copy in copies:
        copy.start()
    for copy in copies:
        copy.wait()
    counts_ref, before_ref, order_ref, kv_ref = held
    block_ref, query_pos_ref, vit_bias_ref, vis_pos_ref = outs
    seq, head = lax.axis_index("seq"), lax.axis_index("head")
    images = counts_ref.shape[0]
    tokens = order_ref.shape[1]
    order = order_ref[...]
    near = lax.broadcasted_iota(jnp.int32, (1, vit_bias_ref.shape[1]), 1)
    first = rows * (2 * head - 1)
    segments = [(0, 0), (rows, first), (2 * rows, -first)]
    near = pick(near, segments) + seq * rows
    own = lax.broadcasted_iota(jnp.int32, (rows, 1), 0) + seq * rows
    vis = lax.broadcasted_iota(jnp.int32, vis_pos_ref.shape, 1)
    if small:
        segments = [(0, seq * merged)]
        for i, k in enumerate(SHIFTS):
            segments.append(((i + 1) * merged, lax.rem(seq - k + seq_count, seq_count) * merged))
        vis = pick(vis, segments)

    def step(i, state):
        pos, near_id, own_id, vis_pos, start, earlier = state
        count, before = counts_ref[i], before_ref[i]
        stop = start + count
        pos = pos + jnp.where(before <= order, count, 0)
        near_id = near_id + jnp.where(near >= 4 * stop, 1, 0)
        own_id = own_id + jnp.where(own >= 4 * stop, 1, 0)
        vis_pos = vis_pos + jnp.where(start <= vis, before - earlier, 0)
        return pos, near_id, own_id, vis_pos, stop, before

    zero = jnp.int32(0)
    state = (order, jnp.zeros_like(near), jnp.zeros_like(own), vis, zero, zero)
    if images <= 32:
        for i in range(images):
            state = step(i, state)
    else:
        state = lax.fori_loop(0, images, step, state)
    pos, near_id, own_id, vis_pos, _, _ = state
    near_id = jnp.where((near >= 0) & (near < rows * seq_count), near_id, -1)
    vit_bias_ref[...] = jnp.where(own_id == near_id, 0.0, masked_score)
    vis_pos_ref[...] = vis_pos.astype(f32)
    row = lax.broadcasted_iota(jnp.int32, (tokens, tokens), 0)
    column = lax.broadcasted_iota(jnp.int32, (tokens, tokens), 1)
    pos_row = pos.astype(f32)
    diagonal = jnp.where(row == column, pos_row, 0.0)
    query_pos_ref[...] = jnp.broadcast_to(jnp.sum(diagonal, axis=1, keepdims=True), query_pos_ref.shape)
    width = kv_ref.shape[2]
    block_ref[:tokens, :width] = kv_ref[:, 0, :]
    block_ref[:tokens, width:] = kv_ref[:, 1, :]
    high = jnp.floor(pos_row * (1.0 / 128.0))
    line = lax.broadcasted_iota(jnp.int32, (8, tokens), 0)
    tail = jnp.where(line == 0, high, jnp.where(line == 1, pos_row - 128.0 * high, 0.0))
    block_ref[tokens:, :tokens] = tail.astype(bf16)
    block_ref[tokens:, tokens:] = jnp.zeros((8, 2 * width - tokens), bf16)


def own_kernel(carried, weight_ref, *refs):
    sources, refs = refs[:carried], refs[carried:]
    q_ref, k_ref, v_ref, wkv_ref = refs[:4]
    kept, (wq, sem) = refs[4:-2], refs[-2:]
    pairs = list(zip(sources[:3], kept[:3]))
    pairs += [(weight_ref.at[j], wq if j == 0 else wkv_ref.at[j - 1]) for j in range(3)]
    pairs += list(zip(sources[3:], kept[3:]))
    copies = [pltpu.make_async_copy(a, b, sem.at[i]) for i, (a, b) in enumerate(pairs)]
    for copy in copies:
        copy.start()
    for copy in copies[:3]:
        copy.wait()
    normed = layer_norm_rows(kept[:1], kept[1], kept[2])
    for j, out_ref in enumerate((q_ref, k_ref, v_ref)):
        copies[3 + j].wait()
        weight = wq[...] if j == 0 else wkv_ref[j - 1]
        out_ref[...] = jnp.dot(normed, weight, preferred_element_type=f32).astype(bf16)
    for copy in copies[6:]:
        copy.wait()


def near_kernel(gain_ref, bias_ref, weight_ref, *refs):
    normed = layer_norm_rows(refs[:-2], gain_ref, bias_ref)
    for j in range(2):
        refs[j - 2][...] = jnp.dot(normed, weight_ref[j], preferred_element_type=f32).astype(bf16)


def vit_kernel(parts, gain_ref, bias_ref, weight_ref, mask_ref, proj_ref, q_ref, *refs):
    key_refs, value_refs = refs[:parts], refs[parts : 2 * parts]
    row_refs = refs[2 * parts : -4]
    out_ref, keys, values, mixed = refs[-4:]
    row = 0
    for key_ref, value_ref in zip(key_refs, value_refs):
        n = key_ref.shape[0]
        keys[row : row + n, :] = key_ref[...]
        values[row : row + n, :] = value_ref[...]
        row += n
    if row_refs:
        normed = layer_norm_rows(row_refs, gain_ref, bias_ref)
        keys[row:, :] = jnp.dot(normed, weight_ref[0], preferred_element_type=f32).astype(bf16)
        values[row:, :] = jnp.dot(normed, weight_ref[1], preferred_element_type=f32).astype(bf16)
    head_cols = q_ref.shape[1]
    factor = math.log2(math.e) / math.sqrt(VIT_HD)
    for h in range(head_cols // VIT_HD):
        first, last = h * VIT_HD, (h + 1) * VIT_HD
        low, high = first // LANES * LANES, -(-last // LANES) * LANES
        column = low + lax.broadcasted_iota(jnp.int32, (1, high - low), 1)
        inside = (column >= first) & (column < last)
        query = jnp.where(inside, q_ref[:, low:high], jnp.zeros((), bf16))
        scores = lax.dot_general(
            query, keys[:, low:high], (((1,), (1,)), ((), ())), preferred_element_type=f32
        )
        scores = scores * factor + mask_ref[...]
        weights = jnp.exp2(scores - jnp.max(scores, axis=1, keepdims=True))
        total = jnp.sum(weights, axis=1, keepdims=True)
        part = jnp.dot(weights.astype(bf16), values[:, low:high], preferred_element_type=f32)
        part = (part * (1.0 / total)).astype(bf16)
        if first == low:
            mixed[:, low:high] = part
        else:
            split = low + LANES
            mixed[:, low:split] = jnp.where(inside[:, :LANES], part[:, :LANES], mixed[:, low:split])
            if high > split:
                mixed[:, split:high] = part[:, LANES:]
    out_ref[...] = jnp.dot(mixed[...], proj_ref[...], preferred_element_type=f32).astype(bf16)


def merge_kernel(rows_ref, mine_ref, other_ref, pbias_ref, gain_ref, bias_ref, weight_ref, out_ref, merged):
    rows, width = rows_ref.shape
    encoded = rows_ref[...].astype(f32) + (mine_ref[...].astype(f32) + other_ref[...].astype(f32))
    encoded = (encoded + pbias_ref[...].reshape(1, width)).astype(bf16).astype(f32)
    normed = layer_norm(encoded, gain_ref[...].reshape(1, width), bias_ref[...].reshape(1, width))
    for c in range(width // LANES):
        merged[c * rows : (c + 1) * rows, :] = normed[:, c * LANES : (c + 1) * LANES]
    total = None
    for i in range(4):
        piece = jnp.concatenate(
            [merged[pl.ds(c * rows + i, rows // 4, stride=4), :] for c in range(width // LANES)], axis=1
        ).astype(bf16)
        term = jnp.dot(piece, weight_ref[i * width : (i + 1) * width, :], preferred_element_type=f32)
        total = term if total is None else total + term
    out_ref[...] = total.astype(bf16)


def attention_kernel(tokens, blocks, chained, final, *refs):
    query_pos_ref, q_ref = refs[:2]
    refs = refs[2:]
    if tokens is None:
        pos_ref, refs = refs[0], refs[1:]
    block_refs, refs = refs[:blocks], refs[blocks:]
    state, refs = (refs[:3], refs[3:]) if chained else (None, refs)
    outs, (kv, va, bias) = refs[:-3], refs[-3:]
    row = 0
    for block_ref in block_refs:
        n = block_ref.shape[0]
        if tokens is None:
            kv[row : row + n, :] = block_ref[...]
            row += n
            continue
        for first in range(0, n, tokens + 8):
            kv[row : row + tokens, :] = block_ref[first : first + tokens, :]
            tail = block_ref[first + tokens : first + tokens + 8, :tokens].astype(f32)
            pos = tail[0:1, :] * 128.0 + tail[1:2, :]
            bias[:, row : row + tokens] = jnp.where(pos <= query_pos_ref[:, :tokens], 0.0, masked_score)
            row += tokens
    count = kv.shape[0]
    if tokens is None:
        bias[...] = jnp.where(pos_ref[...] <= query_pos_ref[:, :1], 0.0, masked_score)
    va[:, HEAD_DIM:] = jnp.ones((count, HEAD_DIM), bf16)
    heads = kv.shape[1] // (2 * HEAD_DIM)
    factor = math.log2(math.e) / math.sqrt(HEAD_DIM)
    for h in range(heads):
        keys = kv[:, h * HEAD_DIM : (h + 1) * HEAD_DIM]
        va[:, :HEAD_DIM] = kv[:, (heads + h) * HEAD_DIM : (heads + h + 1) * HEAD_DIM]
        for g in range(GROUP):
            columns = slice((h * GROUP + g) * HEAD_DIM, (h * GROUP + g + 1) * HEAD_DIM)
            scores = lax.dot_general(
                q_ref[:, columns], keys, (((1,), (1,)), ((), ())), preferred_element_type=f32
            )
            scores = scores * factor + bias[...]
            top = jnp.max(scores, axis=1, keepdims=True)
            if chained:
                wide = jnp.maximum(top, state[1][:, columns])
                copies = -(-count // HEAD_DIM)
                tops = jnp.concatenate([wide] * copies, axis=1)[:, :count] if copies > 1 else wide[:, :count]
                weights = jnp.exp2(scores - tops)
            else:
                wide = jnp.broadcast_to(top, (top.shape[0], HEAD_DIM))
                weights = jnp.exp2(scores - top)
            part = jnp.dot(weights.astype(bf16), va[...], preferred_element_type=f32)
            numer, denom = part[:, :HEAD_DIM], part[:, HEAD_DIM:]
            if chained:
                scale = jnp.exp2(state[1][:, columns] - wide)
                numer = numer + state[0][:, columns] * scale
                denom = denom + state[2][:, columns] * scale
            if final:
                outs[0][:, columns] = (numer / denom).astype(bf16)
            else:
                outs[0][:, columns] = numer
                outs[1][:, columns] = wide
                outs[2][:, columns] = denom


def join_kernel(*refs):
    row = 0
    for ref in refs[:-1]:
        refs[-1][row : row + ref.shape[0], :] = ref[...]
        row += ref.shape[0]


def join(blocks):
    rows = sum(block.shape[0] for block in blocks)
    return vmem_call(
        join_kernel,
        jax.ShapeDtypeStruct((rows, blocks[0].shape[1]), blocks[0].dtype),
        flops=1 << 16,
        nbytes=4 * rows * blocks[0].shape[1],
    )(*blocks)


def attend(query_pos, queries, pos, blocks, state, tokens, final):
    rows, width = queries.shape
    if tokens is None:
        count = sum(block.shape[0] for block in blocks)
        head_args = (query_pos, queries, pos)
    else:
        count = sum(block.shape[0] // (tokens + 8) * tokens for block in blocks)
        head_args = (query_pos, queries)
    wide = jax.ShapeDtypeStruct((rows, width), f32)
    return vmem_call(
        functools.partial(attention_kernel, tokens, len(blocks), state is not None, final),
        jax.ShapeDtypeStruct((rows, width), bf16) if final else (wide, wide, wide),
        scratch=(
            pltpu.VMEM((count, blocks[0].shape[1]), bf16),
            pltpu.VMEM((count, 2 * HEAD_DIM), bf16),
            pltpu.VMEM((rows, count), f32),
        ),
        flops=4 * rows * width * count,
        nbytes=2 * queries.size + 2 * count * blocks[0].shape[1],
        trans=rows * width // HEAD_DIM * count,
        keep=not final,
    )(*head_args, *blocks, *(state or ()))


def per_device(
    patches,
    ln_gain,
    ln_bias,
    qkv_weight,
    proj_weight,
    proj_bias,
    merge_gain,
    merge_bias,
    visual_kv_weight,
    image_tokens,
    text_before,
    text_order,
    queries,
    text_kv,
):
    seq_count = lax.axis_size("seq")
    head_count = lax.axis_size("head")
    patch_rows, model_width = patches.shape
    merged_rows = patch_rows // 4
    head_cols = qkv_weight.shape[2]
    tokens = queries.shape[0]
    kv_width = text_kv.shape[1] * text_kv.shape[2]
    small = is_small(seq_count, head_count)
    near_count = 3 * patch_rows
    share = jax.ShapeDtypeStruct

    ahead = [(2 * i, 2 * i + 2) for i in range(seq_count - 1)]
    back = [(2 * i + 3, 2 * i + 1) for i in range(seq_count - 1)]
    near_first = lax.ppermute(patches, ("seq", "head"), ahead + back)

    block, query_pos, vit_bias, vis_pos = vmem_call(
        functools.partial(prep_kernel, (seq_count, small, patch_rows, merged_rows)),
        (
            share((tokens + 8, kv_width), bf16),
            share((tokens, LANES), f32),
            share((patch_rows, near_count), f32),
            share((1, merged_rows * seq_count), f32),
        ),
        scratch=(
            pltpu.SMEM(image_tokens.shape, jnp.int32),
            pltpu.SMEM(text_before.shape, jnp.int32),
            pltpu.VMEM((1, tokens), jnp.int32),
            pltpu.VMEM(text_kv.shape, bf16),
            pltpu.SemaphoreType.DMA((4,)),
        ),
        spaces={i: pltpu.HBM for i in range(4)},
        flops=1 << 20,
        nbytes=1 << 20,
    )(image_tokens, text_before, text_order[None, :], text_kv)
    pair_swap = [(i, i ^ 1) for i in range(seq_count)]
    jumps = [[(i, (i + 2 * k) % seq_count) for i in range(seq_count)] for k in range(1, seq_count // 2)]
    if small:
        column = [block]
        for jump in jumps:
            column.append(lax.ppermute(block, "seq", jump))
        column.append(lax.ppermute(block, "seq", pair_swap))
        pieces = join(column[1:4])
        column.append(lax.ppermute(pieces, "seq", pair_swap))
        text_blocks = [column]
    else:
        gathered = lax.all_gather(block, "seq", axis=0, tiled=True)
        step = 8 * (tokens + 8)
        text_blocks = [[gathered[i : i + step]] for i in range(0, gathered.shape[0], step)]

    weight = jnp.transpose(qkv_weight, (1, 0, 2))
    cols = share((patch_rows, head_cols), bf16)
    carried = [patches, ln_gain, ln_bias, proj_bias, merge_gain, merge_bias]
    query, key_own, value_own, weight_kv, *carried = vmem_call(
        functools.partial(own_kernel, len(carried)),
        (cols, cols, cols, share((2, model_width, head_cols), bf16), *[share(a.shape, a.dtype) for a in carried]),
        scratch=(pltpu.VMEM((model_width, head_cols), bf16), pltpu.SemaphoreType.DMA((3 + len(carried),))),
        spaces={i: pltpu.HBM for i in range(1 + len(carried))},
        flops=2 * patch_rows * weight.size,
        nbytes=2 * weight.size,
    )(weight, *carried)
    patches, ln_gain, ln_bias, proj_bias, merge_gain, merge_bias = carried

    key_near, value_near = vmem_call(
        near_kernel, (cols, cols), flops=4 * patch_rows * model_width * head_cols, nbytes=2 * weight_kv.size
    )(ln_gain, ln_bias, weight_kv, near_first)
    head_swap = [(0, 1), (1, 0)]
    near_second = lax.ppermute(near_first, "head", head_swap)
    mine_part = vmem_call(
        functools.partial(vit_kernel, 2),
        share((patch_rows, model_width), bf16),
        scratch=(
            pltpu.VMEM((near_count, head_cols), bf16),
            pltpu.VMEM((near_count, head_cols), bf16),
            pltpu.VMEM((patch_rows, head_cols), bf16),
        ),
        flops=4 * patch_rows * near_count * head_cols + 2 * patch_rows * head_cols * model_width,
        nbytes=2 * proj_weight.size,
        trans=patch_rows * near_count * head_cols // VIT_HD,
    )(ln_gain, ln_bias, weight_kv, vit_bias, proj_weight, query, key_own, key_near, value_own, value_near, near_second)
    other_part = lax.ppermute(mine_part, "head", head_swap)
    map_weight = visual_kv_weight.reshape(4 * model_width, -1)
    visual = vmem_call(
        merge_kernel,
        share((merged_rows, kv_width), bf16),
        scratch=(pltpu.VMEM((patch_rows * (model_width // LANES), LANES), f32),),
        flops=2 * merged_rows * map_weight.size,
        nbytes=2 * map_weight.size,
    )(patches, mine_part, other_part, proj_bias, merge_gain, merge_bias, map_weight)

    if small:
        visual_blocks = [[visual]]
        for k in SHIFTS:
            visual_blocks[0].append(lax.ppermute(visual, "seq", [(i, (i + k) % 8) for i in range(8)]))
    else:
        gathered = lax.all_gather(visual, "seq", axis=0, tiled=True)
        step = 8 * merged_rows
        visual_blocks = [[gathered[i : i + step]] for i in range(0, gathered.shape[0], step)]

    state = None
    for text_block in text_blocks:
        state = attend(query_pos, queries, None, text_block, state, tokens, False)
    first = 0
    for i, visual_block in enumerate(visual_blocks):
        count = sum(b.shape[0] for b in visual_block)
        final = i == len(visual_blocks) - 1
        pos = vis_pos[:, first : first + count]
        state = attend(query_pos, queries, pos, visual_block, state, None, final)
        first += count
    return (state, visual.reshape(merged_rows, text_kv.shape[1], -1))


def is_small(seq_count, head_count):
    return seq_count == 8 and head_count == 2


def solution(mesh):
    in_specs = (
        P(("grp", "seq"), None),
        P(),
        P(),
        P(None, None, "head"),
        P("head", None),
        P(),
        P(),
        P(),
        P(None, None, "head"),
        P("grp"),
        P("grp"),
        P(("grp", "seq")),
        P(("grp", "seq"), "head"),
        P(("grp", "seq"), None, "head"),
    )
    out_specs = (P(("grp", "seq"), "head"), P(("grp", "seq"), None, "head"))

    return jax.shard_map(per_device, mesh=mesh, in_specs=in_specs, out_specs=out_specs, check_vma=False)
```

profile of v0, /device:TPU:0, one launch (start us, length us, event | category | flops | bytes accessed | tf_op | source)
XLA Modules:
  0.0 75.4 jit_solution(2950883230434798602)
XLA Ops:
  0.6 5.1 %collective-permute-start = (bf16[192,1280]{1,0:T(8,128)(2,1)}, bf16[192,1280]{1,0:T(8,128)(2,1)S(1)}, u32[]{:S(2)}, u32[]{:S(2)}) collective-permute-start(bf16[192,1280]{1,0:T(8,128)(2,1)} %refs_0_.3), channel_id=1, source_target_pairs={{0,2},{2,4},{4,6},{6,8},{8,10},{10,12},{12,14},{3,1},{5,3},{7,5},{... | collective-permute-start | bytes 1474568 | tf_op jit(solution)/shard_map/ppermute | solution.py:349
  5.7 11.6 %collective-permute-done.refs_0_ = bf16[192,1280]{1,0:T(8,128)(2,1)S(1)} collective-permute-done((bf16[192,1280]{1,0:T(8,128)(2,1)}, bf16[192,1280]{1,0:T(8,128)(2,1)S(1)}, u32[]{:S(2)}, u32[]{:S(2)}) %collective-permute-start) | collective-permute-done | bytes 491552 | tf_op jit(solution)/shard_map/ppermute | solution.py:349
  17.4 1.6 %shard_map.149 = (bf16[136,512]{1,0:T(8,128)(2,1)S(1)}, f32[128,128]{1,0:T(8,128)S(1)}, f32[192,576]{1,0:T(8,128)S(1)}, f32[1,384]{1,0:T(1,128)S(1)}) custom-call(s32[16]{0:T(128)} %refs_0_.2, s32[16]{0:T(128)} %refs_1_.4, s32[1,128]{1,0:T(1,128)} %bitcast.9, bf16[128,2,256]{2,1,0:T(2,128)(2,1)} %refs_3_.2), custom_call_target="tpu_custom_call" | custom-call | flops 1048576 | bytes 1048576 | tf_op jit(solution)/shard_map/pallas_call | solution.py:48
  19.0 0.6 copy-done.3
  19.5 3.4 %shard_map.150 = (bf16[192,640]{1,0:T(8,128)(2,1)S(1)}, bf16[192,640]{1,0:T(8,128)(2,1)S(1)}, bf16[192,640]{1,0:T(8,128)(2,1)S(1)}, bf16[2,1280,640]{2,1,0:T(8,1...) custom-call(bf16[3,1280,640]{2,1,0:T(8,128)(2,1)} %bitcast.8, ...), custom_call_target="tpu_custom_call" | custom-call | flops 943718400 | bytes 4915200 | tf_op jit(solution)/shard_map/pallas_call | solution.py:48
  23.0 0.0 slice-start
  23.0 1.2 %shard_map.151 = (bf16[192,640]{1,0:T(8,128)(2,1)S(1)}, bf16[192,640]{1,0:T(8,128)(2,1)S(1)}) custom-call(f32[1280]{0:T(1024)S(1)} %get-tuple-element.24.gain_ref, f32[1280]{0:T(1024)S(1)} %get-tuple-element.25.bias_ref, bf16[2,1280,640]{2,1,0:T(8,128)(2,1)S(1)} %get-tuple-element.26.weight_ref, bf16[192,1280]{1,0:T(8,128)(2,1)S(1)} %collective-permute-done.refs_0_), custom_call_target="tpu_custom_call" | custom-call | flops 629145600 | bytes 3276800 | tf_op jit(solution)/shard_map/pallas_call | solution.py:48
  24.2 0.0 slice-start.1
  24.2 3.9 %shard_map.152.mine_ref = bf16[192,1280]{1,0:T(8,128)(2,1)S(1)} custom-call(f32[1280]{0:T(1024)S(1)} %get-tuple-element.24.gain_ref, f32[1280]{0:T(1024)S(1)} %get-tuple-element.25.bias_ref, bf16[2,1280,640]{2,1,0:T(8,128)(2,1)S(1)} %get-tuple-element.26.weight_ref, f32[192,576]{1,0:T(8,128)S(1)} %get-tuple-element.27.mask_ref, ...), custom_call_target="tpu_custom_call" | custom-call | flops 597688320 | bytes 1638400 | tf_op jit(solution)/shard_map/pallas_call | solution.py:48
  28.2 0.6 collective-permute-start.2
  28.8 1.6 %collective-permute-start.10 = (bf16[136,512]{1,0:T(8,128)(2,1)S(1)}, bf16[136,512]{1,0:T(8,128)(2,1)S(1)}, u32[]{:S(2)}, u32[]{:S(2)}) collective-permute-start(bf16[136,512]{1,0:T(8,128)(2,1)S(1)} %get-tuple-element.36.refs_2_), channel_id=1, source_target_pairs={{0,4},{2,6},{4,8},{6,10},{8,12},{10,14},{12,0},{14,2},{1,5},{3,7},... | collective-permute-start | bytes 417800 | tf_op jit(solution)/shard_map/ppermute | solution.py:375
  30.3 1.9 %collective-permute-start.11 = (bf16[136,512]{1,0:T(8,128)(2,1)S(1)}, bf16[136,512]{1,0:T(8,128)(2,1)S(1)}, u32[]{:S(2)}, u32[]{:S(2)}) collective-permute-start(bf16[136,512]{1,0:T(8,128)(2,1)S(1)} %get-tuple-element.36.refs_2_), channel_id=1, source_target_pairs={{0,8},{2,10},{4,12},{6,14},{8,0},{10,2},{12,4},{14,6},{1,9},{3,11}... | collective-permute-start | bytes 417800 | tf_op jit(solution)/shard_map/ppermute | solution.py:375
  32.3 2.0 %collective-permute-start.12 = (bf16[136,512]{1,0:T(8,128)(2,1)S(1)}, bf16[136,512]{1,0:T(8,128)(2,1)S(1)}, u32[]{:S(2)}, u32[]{:S(2)}) collective-permute-start(bf16[136,512]{1,0:T(8,128)(2,1)S(1)} %get-tuple-element.36.refs_2_), channel_id=1, source_target_pairs={{0,12},{2,14},{4,0},{6,2},{8,4},{10,6},{12,8},{14,10},{1,13},{3,15... | collective-permute-start | bytes 417800 | tf_op jit(solution)/shard_map/ppermute | solution.py:375
  34.3 2.9 %collective-permute-done.10.refs_0_.refs_3_ = bf16[136,512]{1,0:T(8,128)(2,1)S(1)} collective-permute-done((bf16[136,512]{1,0:T(8,128)(2,1)S(1)}, bf16[136,512]{1,0:T(8,128)(2,1)S(1)}, u32[]{:S(2)}, u32[]{:S(2)}) %collective-permute-start.10) | collective-permute-done | bytes 139296 | tf_op jit(solution)/shard_map/ppermute | solution.py:375
  37.2 5.1 %collective-permute-done.11.refs_1_.refs_4_ = bf16[136,512]{1,0:T(8,128)(2,1)S(1)} collective-permute-done((bf16[136,512]{1,0:T(8,128)(2,1)S(1)}, bf16[136,512]{1,0:T(8,128)(2,1)S(1)}, u32[]{:S(2)}, u32[]{:S(2)}) %collective-permute-start.11) | collective-permute-done | bytes 139296 | tf_op jit(solution)/shard_map/ppermute | solution.py:375
  42.3 2.4 %collective-permute-start.14 = (bf16[408,512]{1,0:T(8,128)(2,1)S(1)}, bf16[408,512]{1,0:T(8,128)(2,1)S(1)}, u32[]{:S(2)}, u32[]{:S(2)}) collective-permute-start(bf16[408,512]{1,0:T(8,128)(2,1)S(1)} %shard_map.154), channel_id=1, source_target_pairs={{0,2},{2,0},{4,6},{6,4},{8,10},{10,8},{12,14},{14,12},{1,3},{3,1},... | collective-permute-start | bytes 1253384 | tf_op jit(solution)/shard_map/ppermute | solution.py:378
  44.8 0.1 collective-permute-start.13
  44.8 0.9 %copy.16 = bf16[640,8,2,256]{3,1,2,0:T(8,128)(2,1)S(1)} copy(bf16[640,8,2,256]{3,2,1,0:T(2,128)(2,1)S(1)} %bitcast.7) | data formatting | bytes 10485760
  45.7 1.5 %shard_map.153.refs_3_ = bf16[48,512]{1,0:T(8,128)(2,1)S(1)} custom-call(bf16[192,1280]{1,0:T(8,128)(2,1)S(1)} %get-tuple-element.23.rows_ref, bf16[192,1280]{1,0:T(8,128)(2,1)S(1)} %shard_map.152.mine_ref, bf16[192,1280]{1,0:T(8,128)(2,1)S(1)} %collective-permute-done.2.other_ref, f32[1280]{0:T(1024)S(1)} %get-tuple-element.33.pbias_ref, ...), custom_call_target="tpu_custom_call" | custom-call | flops 251658240 | bytes 5242880 | tf_op jit(solution)/shard_map/pallas_call | solution.py:48
  47.2 3.5 %collective-permute-start.3 = (bf16[48,512]{1,0:T(8,128)(2,1)S(1)}, bf16[48,512]{1,0:T(8,128)(2,1)S(1)}, u32[]{:S(2)}, u32[]{:S(2)}) collective-permute-start(bf16[48,512]{1,0:T(8,128)(2,1)S(1)} %shard_map.153.refs_3_), channel_id=1, source_target_pairs={{0,4},{2,6},{4,8},{6,10},{8,12},{10,14},{12,0},{14,2},{1,5},{3,7},... | collective-permute-start | bytes 147464 | tf_op jit(solution)/shard_map/ppermute | solution.py:428
  50.7 1.7 %collective-permute-start.4 = (bf16[48,512]{1,0:T(8,128)(2,1)S(1)}, bf16[48,512]{1,0:T(8,128)(2,1)S(1)}, u32[]{:S(2)}, u32[]{:S(2)}) collective-permute-start(bf16[48,512]{1,0:T(8,128)(2,1)S(1)} %shard_map.153.refs_3_), channel_id=1, source_target_pairs={{0,8},{2,10},{4,12},{6,14},{8,0},{10,2},{12,4},{14,6},{1,9},{3,11}... | collective-permute-start | bytes 147464 | tf_op jit(solution)/shard_map/ppermute | solution.py:428
  52.4 0.8 collective-permute-start.5
  53.2 4.3 %collective-permute-done.13.refs_6_ = bf16[136,512]{1,0:T(8,128)(2,1)S(1)} collective-permute-done((bf16[136,512]{1,0:T(8,128)(2,1)S(1)}, bf16[136,512]{1,0:T(8,128)(2,1)S(1)}, u32[]{:S(2)}, u32[]{:S(2)}) %collective-permute-start.13) | collective-permute-done | bytes 139296 | tf_op jit(solution)/shard_map/ppermute | solution.py:376
  57.5 1.7 %collective-permute-start.6 = (bf16[48,512]{1,0:T(8,128)(2,1)S(1)}, bf16[48,512]{1,0:T(8,128)(2,1)S(1)}, u32[]{:S(2)}, u32[]{:S(2)}) collective-permute-start(bf16[48,512]{1,0:T(8,128)(2,1)S(1)} %shard_map.153.refs_3_), channel_id=1, source_target_pairs={{0,2},{2,4},{4,6},{6,8},{8,10},{10,12},{12,14},{14,0},{1,3},{3,5},... | collective-permute-start | bytes 147464 | tf_op jit(solution)/shard_map/ppermute | solution.py:428
  59.2 3.3 %collective-permute-start.7 = (bf16[48,512]{1,0:T(8,128)(2,1)S(1)}, bf16[48,512]{1,0:T(8,128)(2,1)S(1)}, u32[]{:S(2)}, u32[]{:S(2)}) collective-permute-start(bf16[48,512]{1,0:T(8,128)(2,1)S(1)} %shard_map.153.refs_3_), channel_id=1, source_target_pairs={{0,14},{2,0},{4,2},{6,4},{8,6},{10,8},{12,10},{14,12},{1,15},{3,1}... | collective-permute-start | bytes 147464 | tf_op jit(solution)/shard_map/ppermute | solution.py:428
  62.5 1.7 %collective-permute-start.8 = (bf16[48,512]{1,0:T(8,128)(2,1)S(1)}, bf16[48,512]{1,0:T(8,128)(2,1)S(1)}, u32[]{:S(2)}, u32[]{:S(2)}) collective-permute-start(bf16[48,512]{1,0:T(8,128)(2,1)S(1)} %shard_map.153.refs_3_), channel_id=1, source_target_pairs={{0,6},{2,8},{4,10},{6,12},{8,14},{10,0},{12,2},{14,4},{1,7},{3,9},... | collective-permute-start | bytes 147464 | tf_op jit(solution)/shard_map/ppermute | solution.py:428
  64.2 2.1 %collective-permute-start.9 = (bf16[48,512]{1,0:T(8,128)(2,1)S(1)}, bf16[48,512]{1,0:T(8,128)(2,1)}, u32[]{:S(2)}, u32[]{:S(2)}) collective-permute-start(bf16[48,512]{1,0:T(8,128)(2,1)S(1)} %shard_map.153.refs_3_), channel_id=1, source_target_pairs={{0,10},{2,12},{4,14},{6,0},{8,2},{10,4},{12,6},{14,8},{1,11},{3,13... | collective-permute-start | bytes 147464 | tf_op jit(solution)/shard_map/ppermute | solution.py:428
  66.3 3.3 %shard_map.155 = (f32[128,2048]{1,0:T(8,128)S(1)}, f32[128,2048]{1,0:T(8,128)S(1)}, f32[128,2048]{1,0:T(8,128)S(1)}) custom-call(f32[128,128]{1,0:T(8,128)S(1)} %get-tuple-element.21.refs_0_, bf16[128,2048]{1,0:T(8,128)(2,1)S(1)} %copy-done.1, bf16[136,512]{1,0:T(8,128)(2,1)S(1)} %get-tuple-element.36.refs_2_, ...), custom_call_target="tpu_custom_call" | custom-call | flops 1073741824 | bytes 1572864 | tf_op jit(solution)/shard_map/pallas_call | solution.py:48
  69.6 0.6 reshape.11
  70.3 1.0 %copy-done.2 = bf16[128,2048]{1,0:T(8,128)(2,1)S(1)} copy-done((bf16[128,2048]{1,0:T(8,128)(2,1)S(1)}, bf16[128,2048]{1,0:T(8,128)(2,1)}, u32[]{:S(2)}) %copy-start.2) | copy-done | bytes 524312
  71.3 0.7 copy-done.4
  72.0 3.4 %shard_map.156 = bf16[128,2048]{1,0:T(8,128)(2,1)} custom-call(f32[128,128]{1,0:T(8,128)S(1)} %get-tuple-element.21.refs_0_, bf16[128,2048]{1,0:T(8,128)(2,1)S(1)} %copy-done.2, f32[1,384]{1,0:T(1,128)S(1)} %copy-done.4, bf16[48,512]{1,0:T(8,128)(2,1)S(1)} %shard_map.153.refs_3_, bf16[48,512]{1,0:T(8,128)(2,1)S(1)} %collective-permute-done.3.refs_4_, ...), custom_call_target="tpu_custom_call" | custom-call | flops 402653184 | bytes 917504 | tf_op jit(solution)/shard_map/pallas_call | solution.py:48
  (23 shorter events, 0.1 us)
Async XLA Ops:
  0.6 23.6 %copy-start = (bf16[640,1280]{1,0:T(8,128)(2,1)S(1)}, bf16[640,1280]{1,0:T(8,128)(2,1)}, u32[]{:S(2)}) copy-start(bf16[640,1280]{1,0:T(8,128)(2,1)} %proj_ref.1) | copy-start | bytes 4915204
  0.6 16.7 %collective-permute-start = (bf16[192,1280]{1,0:T(8,128)(2,1)}, bf16[192,1280]{1,0:T(8,128)(2,1)S(1)}, u32[]{:S(2)}, u32[]{:S(2)}) collective-permute-start(bf16[192,1280]{1,0:T(8,128)(2,1)} %refs_0_.3), channel_id=1, source_target_pairs={{0,2},{2,4},{4,6},{6,8},{8,10},{10,12},{12,14},{3,1},{5,3},{7,5},{... | collective-permute-start | bytes 1474568 | tf_op jit(solution)/shard_map/ppermute | solution.py:349
  17.4 6.8 %collective-permute-start.1 = (bf16[192,1280]{1,0:T(8,128)(2,1)S(1)}, bf16[192,1280]{1,0:T(8,128)(2,1)S(1)}, u32[]{:S(2)}, u32[]{:S(2)}) collective-permute-start(bf16[192,1280]{1,0:T(8,128)(2,1)S(1)} %collective-permute-done.refs_0_), channel_id=1, source_target_pairs={{0,1},{1,0},{2,3},{3,2},{4,5},{5,4},{6,7},{7,6},{8,9},{9,8},{10,11... | collective-permute-start | bytes 1474568 | tf_op jit(solution)/shard_map/ppermute | solution.py:402
  19.0 0.6 copy-start.3
  23.0 21.8 %slice-start = ((s8[5242880]{0:T(1024)(128)(4,1)}), s8[4194304]{0:T(1024)(128)(4,1)S(1)}, s32[]{:S(2)}) async-start(s8[5242880]{0:T(1024)(128)(4,1)} %bitcast.5), calls=%async_computation | async-start | bytes 8388608
  24.2 20.6 %slice-start.1 = ((s8[5242880]{0:T(1024)(128)(4,1)}), s8[1048576]{0:T(1024)(128)(4,1)S(1)}, s32[]{:S(2)}) async-start(s8[5242880]{0:T(1024)(128)(4,1)} %bitcast.5), calls=%async_computation.1 | async-start | bytes 2097152
  28.2 17.5 %collective-permute-start.2 = (bf16[192,1280]{1,0:T(8,128)(2,1)S(1)}, bf16[192,1280]{1,0:T(8,128)(2,1)S(1)}, u32[]{:S(2)}, u32[]{:S(2)}) collective-permute-start(bf16[192,1280]{1,0:T(8,128)(2,1)S(1)} %shard_map.152.mine_ref), channel_id=1, source_target_pairs={{0,1},{1,0},{2,3},{3,2},{4,5},{5,4},{6,7},{7,6},{8,9},{9,8},{10,11... | collective-permute-start | bytes 1474568 | tf_op jit(solution)/shard_map/ppermute | solution.py:415
  28.8 8.4 %collective-permute-start.10 = (bf16[136,512]{1,0:T(8,128)(2,1)S(1)}, bf16[136,512]{1,0:T(8,128)(2,1)S(1)}, u32[]{:S(2)}, u32[]{:S(2)}) collective-permute-start(bf16[136,512]{1,0:T(8,128)(2,1)S(1)} %get-tuple-element.36.refs_2_), channel_id=1, source_target_pairs={{0,4},{2,6},{4,8},{6,10},{8,12},{10,14},{12,0},{14,2},{1,5},{3,7},... | collective-permute-start | bytes 417800 | tf_op jit(solution)/shard_map/ppermute | solution.py:375
  30.3 11.9 %collective-permute-start.11 = (bf16[136,512]{1,0:T(8,128)(2,1)S(1)}, bf16[136,512]{1,0:T(8,128)(2,1)S(1)}, u32[]{:S(2)}, u32[]{:S(2)}) collective-permute-start(bf16[136,512]{1,0:T(8,128)(2,1)S(1)} %get-tuple-element.36.refs_2_), channel_id=1, source_target_pairs={{0,8},{2,10},{4,12},{6,14},{8,0},{10,2},{12,4},{14,6},{1,9},{3,11}... | collective-permute-start | bytes 417800 | tf_op jit(solution)/shard_map/ppermute | solution.py:375
  32.3 10.0 %collective-permute-start.12 = (bf16[136,512]{1,0:T(8,128)(2,1)S(1)}, bf16[136,512]{1,0:T(8,128)(2,1)S(1)}, u32[]{:S(2)}, u32[]{:S(2)}) collective-permute-start(bf16[136,512]{1,0:T(8,128)(2,1)S(1)} %get-tuple-element.36.refs_2_), channel_id=1, source_target_pairs={{0,12},{2,14},{4,0},{6,2},{8,4},{10,6},{12,8},{14,10},{1,13},{3,15... | collective-permute-start | bytes 417800 | tf_op jit(solution)/shard_map/ppermute | solution.py:375
  42.3 16.9 %collective-permute-start.14 = (bf16[408,512]{1,0:T(8,128)(2,1)S(1)}, bf16[408,512]{1,0:T(8,128)(2,1)S(1)}, u32[]{:S(2)}, u32[]{:S(2)}) collective-permute-start(bf16[408,512]{1,0:T(8,128)(2,1)S(1)} %shard_map.154), channel_id=1, source_target_pairs={{0,2},{2,0},{4,6},{6,4},{8,10},{10,8},{12,14},{14,12},{1,3},{3,1},... | collective-permute-start | bytes 1253384 | tf_op jit(solution)/shard_map/ppermute | solution.py:378
  44.8 12.7 %collective-permute-start.13 = (bf16[136,512]{1,0:T(8,128)(2,1)S(1)}, bf16[136,512]{1,0:T(8,128)(2,1)S(1)}, u32[]{:S(2)}, u32[]{:S(2)}) collective-permute-start(bf16[136,512]{1,0:T(8,128)(2,1)S(1)} %get-tuple-element.36.refs_2_), channel_id=1, source_target_pairs={{0,2},{2,0},{4,6},{6,4},{8,10},{10,8},{12,14},{14,12},{1,3},{3,1},... | collective-permute-start | bytes 417800 | tf_op jit(solution)/shard_map/ppermute | solution.py:376
  45.7 20.6 %copy-start.1 = (bf16[128,2048]{1,0:T(8,128)(2,1)S(1)}, bf16[128,2048]{1,0:T(8,128)(2,1)}, u32[]{:S(2)}) copy-start(bf16[128,2048]{1,0:T(8,128)(2,1)} %refs_1_.7) | copy-start | bytes 1572868
  47.2 15.3 %collective-permute-start.3 = (bf16[48,512]{1,0:T(8,128)(2,1)S(1)}, bf16[48,512]{1,0:T(8,128)(2,1)S(1)}, u32[]{:S(2)}, u32[]{:S(2)}) collective-permute-start(bf16[48,512]{1,0:T(8,128)(2,1)S(1)} %shard_map.153.refs_3_), channel_id=1, source_target_pairs={{0,4},{2,6},{4,8},{6,10},{8,12},{10,14},{12,0},{14,2},{1,5},{3,7},... | collective-permute-start | bytes 147464 | tf_op jit(solution)/shard_map/ppermute | solution.py:428
  50.7 13.5 %collective-permute-start.4 = (bf16[48,512]{1,0:T(8,128)(2,1)S(1)}, bf16[48,512]{1,0:T(8,128)(2,1)S(1)}, u32[]{:S(2)}, u32[]{:S(2)}) collective-permute-start(bf16[48,512]{1,0:T(8,128)(2,1)S(1)} %shard_map.153.refs_3_), channel_id=1, source_target_pairs={{0,8},{2,10},{4,12},{6,14},{8,0},{10,2},{12,4},{14,6},{1,9},{3,11}... | collective-permute-start | bytes 147464 | tf_op jit(solution)/shard_map/ppermute | solution.py:428
  52.4 17.8 %collective-permute-start.5 = (bf16[48,512]{1,0:T(8,128)(2,1)S(1)}, bf16[48,512]{1,0:T(8,128)(2,1)S(1)}, u32[]{:S(2)}, u32[]{:S(2)}) collective-permute-start(bf16[48,512]{1,0:T(8,128)(2,1)S(1)} %shard_map.153.refs_3_), channel_id=1, source_target_pairs={{0,12},{2,14},{4,0},{6,2},{8,4},{10,6},{12,8},{14,10},{1,13},{3,15... | collective-permute-start | bytes 147464 | tf_op jit(solution)/shard_map/ppermute | solution.py:428
  57.5 12.8 %collective-permute-start.6 = (bf16[48,512]{1,0:T(8,128)(2,1)S(1)}, bf16[48,512]{1,0:T(8,128)(2,1)S(1)}, u32[]{:S(2)}, u32[]{:S(2)}) collective-permute-start(bf16[48,512]{1,0:T(8,128)(2,1)S(1)} %shard_map.153.refs_3_), channel_id=1, source_target_pairs={{0,2},{2,4},{4,6},{6,8},{8,10},{10,12},{12,14},{14,0},{1,3},{3,5},... | collective-permute-start | bytes 147464 | tf_op jit(solution)/shard_map/ppermute | solution.py:428
  59.2 11.1 %collective-permute-start.7 = (bf16[48,512]{1,0:T(8,128)(2,1)S(1)}, bf16[48,512]{1,0:T(8,128)(2,1)S(1)}, u32[]{:S(2)}, u32[]{:S(2)}) collective-permute-start(bf16[48,512]{1,0:T(8,128)(2,1)S(1)} %shard_map.153.refs_3_), channel_id=1, source_target_pairs={{0,14},{2,0},{4,2},{6,4},{8,6},{10,8},{12,10},{14,12},{1,15},{3,1}... | collective-permute-start | bytes 147464 | tf_op jit(solution)/shard_map/ppermute | solution.py:428
  62.5 7.8 %collective-permute-start.8 = (bf16[48,512]{1,0:T(8,128)(2,1)S(1)}, bf16[48,512]{1,0:T(8,128)(2,1)S(1)}, u32[]{:S(2)}, u32[]{:S(2)}) collective-permute-start(bf16[48,512]{1,0:T(8,128)(2,1)S(1)} %shard_map.153.refs_3_), channel_id=1, source_target_pairs={{0,6},{2,8},{4,10},{6,12},{8,14},{10,0},{12,2},{14,4},{1,7},{3,9},... | collective-permute-start | bytes 147464 | tf_op jit(solution)/shard_map/ppermute | solution.py:428
  64.2 6.1 %collective-permute-start.9 = (bf16[48,512]{1,0:T(8,128)(2,1)S(1)}, bf16[48,512]{1,0:T(8,128)(2,1)}, u32[]{:S(2)}, u32[]{:S(2)}) collective-permute-start(bf16[48,512]{1,0:T(8,128)(2,1)S(1)} %shard_map.153.refs_3_), channel_id=1, source_target_pairs={{0,10},{2,12},{4,14},{6,0},{8,2},{10,4},{12,6},{14,8},{1,11},{3,13... | collective-permute-start | bytes 147464 | tf_op jit(solution)/shard_map/ppermute | solution.py:428
  70.3 1.0 %copy-start.2 = (bf16[128,2048]{1,0:T(8,128)(2,1)S(1)}, bf16[128,2048]{1,0:T(8,128)(2,1)}, u32[]{:S(2)}) copy-start(bf16[128,2048]{1,0:T(8,128)(2,1)} %refs_1_.7) | copy-start | bytes 1572868
  71.3 0.7 copy-start.4
where the time goes:
time: 75.6 us; the launch traced here: 75.4 us
  starting transfers between devices  28.5 us (38%)
  waiting for transfers between devices  23.9 us (32%)
  Pallas kernels  18.3 us (24%)
  local copies, waits for them, and re-layouts  3.82 us (5%)
  between operations  0.8 us (1%)
    pallas_call x8, Pallas kernels, run(): pl.pallas_call(body, out_shape=jax.tree.map(lambda a: pltpu.VMEM(a.shape,...  18.3 us
    ppermute x7, starting transfers between devices, per_device(): lax.ppermute(visual, 'seq', [(i, (i + k) % 8) for i in range(8)])  14.8 us
    ppermute x1, waiting for transfers between devices, per_device(): near_first = lax.ppermute(patches, ('seq', 'head'), ahead + back)  11.6 us
    ppermute x3, waiting for transfers between devices, per_device(): column.append(lax.ppermute(block, 'seq', jump))  8 us
    ppermute x3, starting transfers between devices, per_device(): column.append(lax.ppermute(block, 'seq', jump))  5.51 us
    ppermute x1, starting transfers between devices, per_device(): near_first = lax.ppermute(patches, ('seq', 'head'), ahead + back)  5.06 us
    ppermute x1, waiting for transfers between devices, per_device(): column.append(lax.ppermute(block, 'seq', pair_swap))  4.28 us
    unnamed x15, local copies, waits for them, and re-layouts  3.18 us
  transfers between devices with their start and end apart: 15, of which 4 were waited for; matrix products, arithmetic and copies ran while one was open for 2% of the time, Pallas kernels for 15%

commit v1 on v0

--- a/solution.py
+++ b/solution.py
@@ -15,7 +15,8 @@
 LANES = 128
 
 epsilon = 1e-06
-SHIFTS = (2, 4, 6, 1, 7, 3, 5)
+
+SHIFTS = (6, 4, 7, 5, 3, 2, 1)
 masked_score = -1e30
 
 
@@ -94,7 +95,7 @@
     if small:
         segments = [(0, seq * merged)]
         for i, k in enumerate(SHIFTS):
-            segments.append(((i + 1) * merged, lax.rem(seq - k + seq_count, seq_count) * merged))
+            segments.append(((i + 1) * merged, lax.bitwise_xor(seq, jnp.int32(k)) * merged))
         vis = pick(vis, segments)
 
     def step(i, state):
@@ -276,6 +277,25 @@
                 outs[2][:, columns] = denom
 
 
+def unpack_kernel(source_ref, out_ref):
+    half = out_ref.shape[2]
+    out_ref[:, 0, :] = source_ref[:, :half]
+    out_ref[:, 1, :] = source_ref[:, half:]
+
+
+def hold(value):
+    spec = pl.BlockSpec(memory_space=pl.ANY)
+    return pl.pallas_call(
+        lambda source, target: None,
+        out_shape=jax.ShapeDtypeStruct(value.shape, value.dtype),
+        in_specs=[spec],
+        out_specs=spec,
+        input_output_aliases={0: 0},
+        compiler_params=pltpu.CompilerParams(vmem_limit_bytes=1 << 20),
+        name="hold",
+    )(value)
+
+
 def join_kernel(*refs):
     row = 0
     for ref in refs[:-1]:
@@ -368,7 +388,7 @@
         nbytes=1 << 20,
     )(image_tokens, text_before, text_order[None, :], text_kv)
     pair_swap = [(i, i ^ 1) for i in range(seq_count)]
-    jumps = [[(i, (i + 2 * k) % seq_count) for i in range(seq_count)] for k in range(1, seq_count // 2)]
+    jumps = [[(i, i ^ (2 * k)) for i in range(seq_count)] for k in range(1, seq_count // 2)]
     if small:
         column = [block]
         for jump in jumps:
@@ -413,7 +433,7 @@
         trans=patch_rows * near_count * head_cols // VIT_HD,
     )(ln_gain, ln_bias, weight_kv, vit_bias, proj_weight, query, key_own, key_near, value_own, value_near, near_second)
     other_part = lax.ppermute(mine_part, "head", head_swap)
-    map_weight = visual_kv_weight.reshape(4 * model_width, -1)
+    map_weight = hold(visual_kv_weight.reshape(4 * model_width, -1))
     visual = vmem_call(
         merge_kernel,
         share((merged_rows, kv_width), bf16),
@@ -425,12 +445,13 @@
     if small:
         visual_blocks = [[visual]]
         for k in SHIFTS:
-            visual_blocks[0].append(lax.ppermute(visual, "seq", [(i, (i + k) % 8) for i in range(8)]))
+            visual_blocks[0].append(lax.ppermute(visual, "seq", [(i, i ^ k) for i in range(seq_count)]))
     else:
         gathered = lax.all_gather(visual, "seq", axis=0, tiled=True)
         step = 8 * merged_rows
         visual_blocks = [[gathered[i : i + step]] for i in range(0, gathered.shape[0], step)]
 
+    visual_out = vmem_call(unpack_kernel, share((merged_rows,) + text_kv.shape[1:], bf16), flops=1 << 16)(visual)
     state = None
     for text_block in text_blocks:
         state = attend(query_pos, queries, None, text_block, state, tokens, False)
@@ -441,7 +462,7 @@
         pos = vis_pos[:, first : first + count]
         state = attend(query_pos, queries, pos, visual_block, state, None, final)
         first += count
-    return (state, visual.reshape(merged_rows, text_kv.shape[1], -1))
+    return (state, visual_out)
 
 
 def is_small(seq_count, head_count):

time: 75.6 us -> 73.6 us (0.974)
  local copies, waits for them, and re-layouts: 3.82 us -> 1.18 us
  starting transfers between devices: 28.5 us -> 30.1 us
  waiting for transfers between devices: 23.9 us -> 23 us
    ppermute x1, waiting for transfers between devices: 4.28 us -> 0.69 us  [per_device(): column.append(lax.ppermute(block, 'seq', pair_swap))]
    ppermute x7, starting transfers between devices: 14.8 us -> 17.5 us  [per_device(): lax.ppermute(visual, 'seq', [(i, i ^ k) for i in range(seq_count)])]
    ppermute x3, waiting for transfers between devices: 8 us -> 10.6 us  [per_device(): column.append(lax.ppermute(block, 'seq', jump))]
    unnamed x15 -> x9, local copies, waits for them, and re-layouts: 3.18 us -> 1.18 us
    ppermute x3, starting transfers between devices: 5.51 us -> 4.39 us  [per_device(): column.append(lax.ppermute(block, 'seq', jump))]
    pallas_call x8 -> x9, Pallas kernels: 18.3 us -> 18.4 us  [run(): pl.pallas_call(body, out_shape=jax.tree.map(lambda a: pltpu.VMEM(a.shape,...]
  transfers between devices with their start and end apart: 15 -> 15, of which waited for: 4 -> 4; matrix products, arithmetic and copies ran while one was open for 2% -> 2% of each run, Pallas kernels for 15% -> 16%
where the time goes in v1:
time: 73.6 us; the launch traced here: 73.5 us
  starting transfers between devices  30.1 us (41%)
  waiting for transfers between devices  23 us (31%)
  Pallas kernels  18.4 us (25%)
  local copies, waits for them, and re-layouts  1.18 us (2%)
  between operations  0.79 us (1%)
    pallas_call x9, Pallas kernels, run(): pl.pallas_call(body, out_shape=jax.tree.map(lambda a: pltpu.VMEM(a.shape,...  18.4 us
    ppermute x7, starting transfers between devices, per_device(): lax.ppermute(visual, 'seq', [(i, i ^ k) for i in range(seq_count)])  17.5 us
    ppermute x1, waiting for transfers between devices, per_device(): near_first = lax.ppermute(patches, ('seq', 'head'), ahead + back)  11.6 us
    ppermute x3, waiting for transfers between devices, per_device(): column.append(lax.ppermute(block, 'seq', jump))  10.6 us
    ppermute x1, starting transfers between devices, per_device(): near_first = lax.ppermute(patches, ('seq', 'head'), ahead + back)  5.06 us
    ppermute x3, starting transfers between devices, per_device(): column.append(lax.ppermute(block, 'seq', jump))  4.39 us
    ppermute x1, starting transfers between devices, per_device(): column.append(lax.ppermute(pieces, 'seq', pair_swap))  2.44 us
  transfers between devices with their start and end apart: 15, of which 4 were waited for; matrix products, arithmetic and copies ran while one was open for 2% of the time, Pallas kernels for 16%

profile of v1, /device:TPU:0, one launch (start us, length us, event | category | flops | bytes accessed | tf_op | source)
XLA Modules:
  0.0 73.5 jit_solution(5338397710655571516)
XLA Ops:
  0.6 5.1 %collective-permute-start = (bf16[192,1280]{1,0:T(8,128)(2,1)}, bf16[192,1280]{1,0:T(8,128)(2,1)S(1)}, u32[]{:S(2)}, u32[]{:S(2)}) collective-permute-start(bf16[192,1280]{1,0:T(8,128)(2,1)} %refs_0_.3), channel_id=1, source_target_pairs={{0,2},{2,4},{4,6},{6,8},{8,10},{10,12},{12,14},{3,1},{5,3},{7,5},{... | collective-permute-start | bytes 1474568 | tf_op jit(solution)/shard_map/ppermute | solution.py:369
  5.7 11.6 %collective-permute-done.refs_0_ = bf16[192,1280]{1,0:T(8,128)(2,1)S(1)} collective-permute-done((bf16[192,1280]{1,0:T(8,128)(2,1)}, bf16[192,1280]{1,0:T(8,128)(2,1)S(1)}, u32[]{:S(2)}, u32[]{:S(2)}) %collective-permute-start) | collective-permute-done | bytes 491552 | tf_op jit(solution)/shard_map/ppermute | solution.py:369
  17.4 0.0 collective-permute-start.1
  17.4 1.6 %shard_map.149 = (bf16[136,512]{1,0:T(8,128)(2,1)S(1)}, f32[128,128]{1,0:T(8,128)S(1)}, f32[192,576]{1,0:T(8,128)S(1)}, f32[1,384]{1,0:T(1,128)S(1)}) custom-call(s32[16]{0:T(128)} %refs_0_.2, s32[16]{0:T(128)} %refs_1_.4, s32[1,128]{1,0:T(1,128)} %bitcast.9, bf16[128,2,256]{2,1,0:T(2,128)(2,1)} %refs_3_.2), custom_call_target="tpu_custom_call" | custom-call | flops 1048576 | bytes 1048576 | tf_op jit(solution)/shard_map/pallas_call | solution.py:49
  19.0 3.5 %shard_map.150 = (bf16[192,640]{1,0:T(8,128)(2,1)S(1)}, bf16[192,640]{1,0:T(8,128)(2,1)S(1)}, bf16[192,640]{1,0:T(8,128)(2,1)S(1)}, bf16[2,1280,640]{2,1,0:T(8,1...) custom-call(bf16[3,1280,640]{2,1,0:T(8,128)(2,1)} %bitcast.8, ...), custom_call_target="tpu_custom_call" | custom-call | flops 943718400 | bytes 4915200 | tf_op jit(solution)/shard_map/pallas_call | solution.py:49
  22.4 0.0 slice-start
  22.5 1.2 %shard_map.151 = (bf16[192,640]{1,0:T(8,128)(2,1)S(1)}, bf16[192,640]{1,0:T(8,128)(2,1)S(1)}) custom-call(f32[1280]{0:T(1024)S(1)} %get-tuple-element.24.gain_ref, f32[1280]{0:T(1024)S(1)} %get-tuple-element.25.bias_ref, bf16[2,1280,640]{2,1,0:T(8,128)(2,1)S(1)} %get-tuple-element.26.weight_ref, bf16[192,1280]{1,0:T(8,128)(2,1)S(1)} %collective-permute-done.refs_0_), custom_call_target="tpu_custom_call" | custom-call | flops 629145600 | bytes 3276800 | tf_op jit(solution)/shard_map/pallas_call | solution.py:49
  23.6 0.0 collective-permute-done.1.refs_4_
  23.7 0.0 slice-start.1
  23.7 4.0 %shard_map.152.mine_ref = bf16[192,1280]{1,0:T(8,128)(2,1)S(1)} custom-call(f32[1280]{0:T(1024)S(1)} %get-tuple-element.24.gain_ref, f32[1280]{0:T(1024)S(1)} %get-tuple-element.25.bias_ref, bf16[2,1280,640]{2,1,0:T(8,128)(2,1)S(1)} %get-tuple-element.26.weight_ref, f32[192,576]{1,0:T(8,128)S(1)} %get-tuple-element.27.mask_ref, ...), custom_call_target="tpu_custom_call" | custom-call | flops 597688320 | bytes 1638400 | tf_op jit(solution)/shard_map/pallas_call | solution.py:49
  27.6 0.6 collective-permute-start.2
  28.2 1.6 %collective-permute-start.10 = (bf16[136,512]{1,0:T(8,128)(2,1)S(1)}, bf16[136,512]{1,0:T(8,128)(2,1)S(1)}, u32[]{:S(2)}, u32[]{:S(2)}) collective-permute-start(bf16[136,512]{1,0:T(8,128)(2,1)S(1)} %get-tuple-element.36.refs_2_), channel_id=1, source_target_pairs={{0,4},{2,6},{4,0},{6,2},{8,12},{10,14},{12,8},{14,10},{1,5},{3,7},... | collective-permute-start | bytes 417800 | tf_op jit(solution)/shard_map/ppermute | solution.py:395
  29.8 1.9 %collective-permute-start.11 = (bf16[136,512]{1,0:T(8,128)(2,1)S(1)}, bf16[136,512]{1,0:T(8,128)(2,1)S(1)}, u32[]{:S(2)}, u32[]{:S(2)}) collective-permute-start(bf16[136,512]{1,0:T(8,128)(2,1)S(1)} %get-tuple-element.36.refs_2_), channel_id=1, source_target_pairs={{0,8},{2,10},{4,12},{6,14},{8,0},{10,2},{12,4},{14,6},{1,9},{3,11}... | collective-permute-start | bytes 417800 | tf_op jit(solution)/shard_map/ppermute | solution.py:395
  31.7 0.9 %collective-permute-start.12 = (bf16[136,512]{1,0:T(8,128)(2,1)S(1)}, bf16[136,512]{1,0:T(8,128)(2,1)S(1)}, u32[]{:S(2)}, u32[]{:S(2)}) collective-permute-start(bf16[136,512]{1,0:T(8,128)(2,1)S(1)} %get-tuple-element.36.refs_2_), channel_id=1, source_target_pairs={{0,12},{2,14},{4,8},{6,10},{8,4},{10,6},{12,0},{14,2},{1,13},{3,15... | collective-permute-start | bytes 417800 | tf_op jit(solution)/shard_map/ppermute | solution.py:395
  32.6 3.4 %collective-permute-done.10.refs_0_.refs_3_ = bf16[136,512]{1,0:T(8,128)(2,1)S(1)} collective-permute-done((bf16[136,512]{1,0:T(8,128)(2,1)S(1)}, bf16[136,512]{1,0:T(8,128)(2,1)S(1)}, u32[]{:S(2)}, u32[]{:S(2)}) %collective-permute-start.10) | collective-permute-done | bytes 139296 | tf_op jit(solution)/shard_map/ppermute | solution.py:395
  36.0 7.2 %collective-permute-done.11.refs_1_.refs_4_ = bf16[136,512]{1,0:T(8,128)(2,1)S(1)} collective-permute-done((bf16[136,512]{1,0:T(8,128)(2,1)S(1)}, bf16[136,512]{1,0:T(8,128)(2,1)S(1)}, u32[]{:S(2)}, u32[]{:S(2)}) %collective-permute-start.11) | collective-permute-done | bytes 139296 | tf_op jit(solution)/shard_map/ppermute | solution.py:395
  43.2 0.0 collective-permute-done.12.refs_2_.refs_5_
  43.2 2.4 %collective-permute-start.14 = (bf16[408,512]{1,0:T(8,128)(2,1)S(1)}, bf16[408,512]{1,0:T(8,128)(2,1)S(1)}, u32[]{:S(2)}, u32[]{:S(2)}) collective-permute-start(bf16[408,512]{1,0:T(8,128)(2,1)S(1)} %shard_map.154), channel_id=1, source_target_pairs={{0,2},{2,0},{4,6},{6,4},{8,10},{10,8},{12,14},{14,12},{1,3},{3,1},... | collective-permute-start | bytes 1253384 | tf_op jit(solution)/shard_map/ppermute | solution.py:398
  45.7 0.1 collective-permute-start.13
  45.8 1.2 %copy.17 = bf16[640,8,2,256]{3,1,2,0:T(8,128)(2,1)S(1)} copy(bf16[640,8,2,256]{3,2,1,0:T(2,128)(2,1)S(1)} %bitcast.7) | data formatting | bytes 10485760
  46.9 0.0 copy-start.1
  47.0 1.5 %shard_map.153.refs_3_.source_ref = bf16[48,512]{1,0:T(8,128)(2,1)S(1)} custom-call(bf16[192,1280]{1,0:T(8,128)(2,1)S(1)} %get-tuple-element.23.rows_ref, bf16[192,1280]{1,0:T(8,128)(2,1)S(1)} %shard_map.152.mine_ref, bf16[192,1280]{1,0:T(8,128)(2,1)S(1)} %collective-permute-done.2.other_ref, f32[1280]{0:T(1024)S(1)} %get-tuple-element.33.pbias_ref, ...), custom_call_target="tpu_custom_call" | custom-call | flops 251658240 | bytes 5242880 | tf_op jit(solution)/shard_map/pallas_call | solution.py:49
  48.5 2.3 %collective-permute-start.3 = (bf16[48,512]{1,0:T(8,128)(2,1)S(1)}, bf16[48,512]{1,0:T(8,128)(2,1)S(1)}, u32[]{:S(2)}, u32[]{:S(2)}) collective-permute-start(bf16[48,512]{1,0:T(8,128)(2,1)S(1)} %shard_map.153.refs_3_.source_ref), channel_id=1, source_target_pairs={{0,12},{2,14},{4,8},{6,10},{8,4},{10,6},{12,0},{14,2},{1,13},{3,15... | collective-permute-start | bytes 147464 | tf_op jit(solution)/shard_map/ppermute | solution.py:448
  50.8 1.6 %collective-permute-start.4 = (bf16[48,512]{1,0:T(8,128)(2,1)S(1)}, bf16[48,512]{1,0:T(8,128)(2,1)S(1)}, u32[]{:S(2)}, u32[]{:S(2)}) collective-permute-start(bf16[48,512]{1,0:T(8,128)(2,1)S(1)} %shard_map.153.refs_3_.source_ref), channel_id=1, source_target_pairs={{0,8},{2,10},{4,12},{6,14},{8,0},{10,2},{12,4},{14,6},{1,9},{3,11}... | collective-permute-start | bytes 147464 | tf_op jit(solution)/shard_map/ppermute | solution.py:448
  52.4 3.8 %collective-permute-start.5 = (bf16[48,512]{1,0:T(8,128)(2,1)S(1)}, bf16[48,512]{1,0:T(8,128)(2,1)S(1)}, u32[]{:S(2)}, u32[]{:S(2)}) collective-permute-start(bf16[48,512]{1,0:T(8,128)(2,1)S(1)} %shard_map.153.refs_3_.source_ref), channel_id=1, source_target_pairs={{0,14},{2,12},{4,10},{6,8},{8,6},{10,4},{12,2},{14,0},{1,15},{3,13... | collective-permute-start | bytes 147464 | tf_op jit(solution)/shard_map/ppermute | solution.py:448
  56.2 0.7 collective-permute-done.13.refs_6_
  56.9 6.3 %collective-permute-start.6 = (bf16[48,512]{1,0:T(8,128)(2,1)S(1)}, bf16[48,512]{1,0:T(8,128)(2,1)S(1)}, u32[]{:S(2)}, u32[]{:S(2)}) collective-permute-start(bf16[48,512]{1,0:T(8,128)(2,1)S(1)} %shard_map.153.refs_3_.source_ref), channel_id=1, source_target_pairs={{0,10},{2,8},{4,14},{6,12},{8,2},{10,0},{12,6},{14,4},{1,11},{3,9}... | collective-permute-start | bytes 147464 | tf_op jit(solution)/shard_map/ppermute | solution.py:448
  63.2 1.7 %collective-permute-start.8 = (bf16[48,512]{1,0:T(8,128)(2,1)S(1)}, bf16[48,512]{1,0:T(8,128)(2,1)S(1)}, u32[]{:S(2)}, u32[]{:S(2)}) collective-permute-start(bf16[48,512]{1,0:T(8,128)(2,1)S(1)} %shard_map.153.refs_3_.source_ref), channel_id=1, source_target_pairs={{0,4},{2,6},{4,0},{6,2},{8,12},{10,14},{12,8},{14,10},{1,5},{3,7},... | collective-permute-start | bytes 147464 | tf_op jit(solution)/shard_map/ppermute | solution.py:448
  65.0 1.7 %collective-permute-start.9 = (bf16[48,512]{1,0:T(8,128)(2,1)S(1)}, bf16[48,512]{1,0:T(8,128)(2,1)S(1)}, u32[]{:S(2)}, u32[]{:S(2)}) collective-permute-start(bf16[48,512]{1,0:T(8,128)(2,1)S(1)} %shard_map.153.refs_3_.source_ref), channel_id=1, source_target_pairs={{0,2},{2,0},{4,6},{6,4},{8,10},{10,8},{12,14},{14,12},{1,3},{3,1},... | collective-permute-start | bytes 147464 | tf_op jit(solution)/shard_map/ppermute | solution.py:448
  66.7 3.4 %shard_map.155 = (f32[128,2048]{1,0:T(8,128)S(1)}, f32[128,2048]{1,0:T(8,128)S(1)}, f32[128,2048]{1,0:T(8,128)S(1)}) custom-call(f32[128,128]{1,0:T(8,128)S(1)} %get-tuple-element.21.refs_0_, bf16[128,2048]{1,0:T(8,128)(2,1)S(1)} %copy-done.1, bf16[136,512]{1,0:T(8,128)(2,1)S(1)} %get-tuple-element.36.refs_2_, ...), custom_call_target="tpu_custom_call" | custom-call | flops 1073741824 | bytes 1572864 | tf_op jit(solution)/shard_map/pallas_call | solution.py:49
  70.2 0.7 shard_map.157
  70.9 2.6 %shard_map.156 = bf16[128,2048]{1,0:T(8,128)(2,1)} custom-call(f32[128,128]{1,0:T(8,128)S(1)} %get-tuple-element.21.refs_0_, bf16[128,2048]{1,0:T(8,128)(2,1)S(1)} %copy-done.1, f32[1,384]{1,0:T(1,128)S(1)} %get-tuple-element.22.refs_2_, bf16[48,512]{1,0:T(8,128)(2,1)S(1)} %shard_map.153.refs_3_.source_ref, ...), custom_call_target="tpu_custom_call" | custom-call | flops 402653184 | bytes 917504 | tf_op jit(solution)/shard_map/pallas_call | solution.py:49
  (18 shorter events, 0.1 us)
Async XLA Ops:
  0.6 23.0 %copy-start = (bf16[640,1280]{1,0:T(8,128)(2,1)S(1)}, bf16[640,1280]{1,0:T(8,128)(2,1)}, u32[]{:S(2)}) copy-start(bf16[640,1280]{1,0:T(8,128)(2,1)} %proj_ref.1) | copy-start | bytes 4915204
  0.6 16.7 %collective-permute-start = (bf16[192,1280]{1,0:T(8,128)(2,1)}, bf16[192,1280]{1,0:T(8,128)(2,1)S(1)}, u32[]{:S(2)}, u32[]{:S(2)}) collective-permute-start(bf16[192,1280]{1,0:T(8,128)(2,1)} %refs_0_.3), channel_id=1, source_target_pairs={{0,2},{2,4},{4,6},{6,8},{8,10},{10,12},{12,14},{3,1},{5,3},{7,5},{... | collective-permute-start | bytes 1474568 | tf_op jit(solution)/shard_map/ppermute | solution.py:369
  17.4 6.3 %collective-permute-start.1 = (bf16[192,1280]{1,0:T(8,128)(2,1)S(1)}, bf16[192,1280]{1,0:T(8,128)(2,1)S(1)}, u32[]{:S(2)}, u32[]{:S(2)}) collective-permute-start(bf16[192,1280]{1,0:T(8,128)(2,1)S(1)} %collective-permute-done.refs_0_), channel_id=1, source_target_pairs={{0,1},{1,0},{2,3},{3,2},{4,5},{5,4},{6,7},{7,6},{8,9},{9,8},{10,11... | collective-permute-start | bytes 1474568 | tf_op jit(solution)/shard_map/ppermute | solution.py:422
  22.4 23.3 %slice-start = ((s8[5242880]{0:T(1024)(128)(4,1)}), s8[4194304]{0:T(1024)(128)(4,1)S(1)}, s32[]{:S(2)}) async-start(s8[5242880]{0:T(1024)(128)(4,1)} %bitcast.5), calls=%async_computation | async-start | bytes 8388608
  23.7 22.1 %slice-start.1 = ((s8[5242880]{0:T(1024)(128)(4,1)}), s8[1048576]{0:T(1024)(128)(4,1)S(1)}, s32[]{:S(2)}) async-start(s8[5242880]{0:T(1024)(128)(4,1)} %bitcast.5), calls=%async_computation.1 | async-start | bytes 2097152
  27.6 19.3 %collective-permute-start.2 = (bf16[192,1280]{1,0:T(8,128)(2,1)S(1)}, bf16[192,1280]{1,0:T(8,128)(2,1)S(1)}, u32[]{:S(2)}, u32[]{:S(2)}) collective-permute-start(bf16[192,1280]{1,0:T(8,128)(2,1)S(1)} %shard_map.152.mine_ref), channel_id=1, source_target_pairs={{0,1},{1,0},{2,3},{3,2},{4,5},{5,4},{6,7},{7,6},{8,9},{9,8},{10,11... | collective-permute-start | bytes 1474568 | tf_op jit(solution)/shard_map/ppermute | solution.py:435
  28.2 7.8 %collective-permute-start.10 = (bf16[136,512]{1,0:T(8,128)(2,1)S(1)}, bf16[136,512]{1,0:T(8,128)(2,1)S(1)}, u32[]{:S(2)}, u32[]{:S(2)}) collective-permute-start(bf16[136,512]{1,0:T(8,128)(2,1)S(1)} %get-tuple-element.36.refs_2_), channel_id=1, source_target_pairs={{0,4},{2,6},{4,0},{6,2},{8,12},{10,14},{12,8},{14,10},{1,5},{3,7},... | collective-permute-start | bytes 417800 | tf_op jit(solution)/shard_map/ppermute | solution.py:395
  29.8 13.4 %collective-permute-start.11 = (bf16[136,512]{1,0:T(8,128)(2,1)S(1)}, bf16[136,512]{1,0:T(8,128)(2,1)S(1)}, u32[]{:S(2)}, u32[]{:S(2)}) collective-permute-start(bf16[136,512]{1,0:T(8,128)(2,1)S(1)} %get-tuple-element.36.refs_2_), channel_id=1, source_target_pairs={{0,8},{2,10},{4,12},{6,14},{8,0},{10,2},{12,4},{14,6},{1,9},{3,11}... | collective-permute-start | bytes 417800 | tf_op jit(solution)/shard_map/ppermute | solution.py:395
  31.7 11.5 %collective-permute-start.12 = (bf16[136,512]{1,0:T(8,128)(2,1)S(1)}, bf16[136,512]{1,0:T(8,128)(2,1)S(1)}, u32[]{:S(2)}, u32[]{:S(2)}) collective-permute-start(bf16[136,512]{1,0:T(8,128)(2,1)S(1)} %get-tuple-element.36.refs_2_), channel_id=1, source_target_pairs={{0,12},{2,14},{4,8},{6,10},{8,4},{10,6},{12,0},{14,2},{1,13},{3,15... | collective-permute-start | bytes 417800 | tf_op jit(solution)/shard_map/ppermute | solution.py:395
  43.2 20.0 %collective-permute-start.14 = (bf16[408,512]{1,0:T(8,128)(2,1)S(1)}, bf16[408,512]{1,0:T(8,128)(2,1)S(1)}, u32[]{:S(2)}, u32[]{:S(2)}) collective-permute-start(bf16[408,512]{1,0:T(8,128)(2,1)S(1)} %shard_map.154), channel_id=1, source_target_pairs={{0,2},{2,0},{4,6},{6,4},{8,10},{10,8},{12,14},{14,12},{1,3},{3,1},... | collective-permute-start | bytes 1253384 | tf_op jit(solution)/shard_map/ppermute | solution.py:398
  45.7 11.2 %collective-permute-start.13 = (bf16[136,512]{1,0:T(8,128)(2,1)S(1)}, bf16[136,512]{1,0:T(8,128)(2,1)S(1)}, u32[]{:S(2)}, u32[]{:S(2)}) collective-permute-start(bf16[136,512]{1,0:T(8,128)(2,1)S(1)} %get-tuple-element.36.refs_2_), channel_id=1, source_target_pairs={{0,2},{2,0},{4,6},{6,4},{8,10},{10,8},{12,14},{14,12},{1,3},{3,1},... | collective-permute-start | bytes 417800 | tf_op jit(solution)/shard_map/ppermute | solution.py:396
  46.9 19.8 %copy-start.1 = (bf16[128,2048]{1,0:T(8,128)(2,1)S(1)}, bf16[128,2048]{1,0:T(8,128)(2,1)}, u32[]{:S(2)}) copy-start(bf16[128,2048]{1,0:T(8,128)(2,1)} %refs_1_.7) | copy-start | bytes 1572868
  48.5 14.7 %collective-permute-start.3 = (bf16[48,512]{1,0:T(8,128)(2,1)S(1)}, bf16[48,512]{1,0:T(8,128)(2,1)S(1)}, u32[]{:S(2)}, u32[]{:S(2)}) collective-permute-start(bf16[48,512]{1,0:T(8,128)(2,1)S(1)} %shard_map.153.refs_3_.source_ref), channel_id=1, source_target_pairs={{0,12},{2,14},{4,8},{6,10},{8,4},{10,6},{12,0},{14,2},{1,13},{3,15... | collective-permute-start | bytes 147464 | tf_op jit(solution)/shard_map/ppermute | solution.py:448
  50.8 14.2 %collective-permute-start.4 = (bf16[48,512]{1,0:T(8,128)(2,1)S(1)}, bf16[48,512]{1,0:T(8,128)(2,1)S(1)}, u32[]{:S(2)}, u32[]{:S(2)}) collective-permute-start(bf16[48,512]{1,0:T(8,128)(2,1)S(1)} %shard_map.153.refs_3_.source_ref), channel_id=1, source_target_pairs={{0,8},{2,10},{4,12},{6,14},{8,0},{10,2},{12,4},{14,6},{1,9},{3,11}... | collective-permute-start | bytes 147464 | tf_op jit(solution)/shard_map/ppermute | solution.py:448
  52.4 18.4 %collective-permute-start.5 = (bf16[48,512]{1,0:T(8,128)(2,1)S(1)}, bf16[48,512]{1,0:T(8,128)(2,1)S(1)}, u32[]{:S(2)}, u32[]{:S(2)}) collective-permute-start(bf16[48,512]{1,0:T(8,128)(2,1)S(1)} %shard_map.153.refs_3_.source_ref), channel_id=1, source_target_pairs={{0,14},{2,12},{4,10},{6,8},{8,6},{10,4},{12,2},{14,0},{1,15},{3,13... | collective-permute-start | bytes 147464 | tf_op jit(solution)/shard_map/ppermute | solution.py:448
  56.9 13.9 %collective-permute-start.6 = (bf16[48,512]{1,0:T(8,128)(2,1)S(1)}, bf16[48,512]{1,0:T(8,128)(2,1)S(1)}, u32[]{:S(2)}, u32[]{:S(2)}) collective-permute-start(bf16[48,512]{1,0:T(8,128)(2,1)S(1)} %shard_map.153.refs_3_.source_ref), channel_id=1, source_target_pairs={{0,10},{2,8},{4,14},{6,12},{8,2},{10,0},{12,6},{14,4},{1,11},{3,9}... | collective-permute-start | bytes 147464 | tf_op jit(solution)/shard_map/ppermute | solution.py:448
  63.2 7.6 %collective-permute-start.7 = (bf16[48,512]{1,0:T(8,128)(2,1)S(1)}, bf16[48,512]{1,0:T(8,128)(2,1)S(1)}, u32[]{:S(2)}, u32[]{:S(2)}) collective-permute-start(bf16[48,512]{1,0:T(8,128)(2,1)S(1)} %shard_map.153.refs_3_.source_ref), channel_id=1, source_target_pairs={{0,6},{2,4},{4,2},{6,0},{8,14},{10,12},{12,10},{14,8},{1,7},{3,5},... | collective-permute-start | bytes 147464 | tf_op jit(solution)/shard_map/ppermute | solution.py:448
  63.2 7.6 %collective-permute-start.8 = (bf16[48,512]{1,0:T(8,128)(2,1)S(1)}, bf16[48,512]{1,0:T(8,128)(2,1)S(1)}, u32[]{:S(2)}, u32[]{:S(2)}) collective-permute-start(bf16[48,512]{1,0:T(8,128)(2,1)S(1)} %shard_map.153.refs_3_.source_ref), channel_id=1, source_target_pairs={{0,4},{2,6},{4,0},{6,2},{8,12},{10,14},{12,8},{14,10},{1,5},{3,7},... | collective-permute-start | bytes 147464 | tf_op jit(solution)/shard_map/ppermute | solution.py:448
  65.0 5.9 %collective-permute-start.9 = (bf16[48,512]{1,0:T(8,128)(2,1)S(1)}, bf16[48,512]{1,0:T(8,128)(2,1)S(1)}, u32[]{:S(2)}, u32[]{:S(2)}) collective-permute-start(bf16[48,512]{1,0:T(8,128)(2,1)S(1)} %shard_map.153.refs_3_.source_ref), channel_id=1, source_target_pairs={{0,2},{2,0},{4,6},{6,4},{8,10},{10,8},{12,14},{14,12},{1,3},{3,1},... | collective-permute-start | bytes 147464 | tf_op jit(solution)/shard_map/ppermute | solution.py:448
